TPU v7x, 128 devices: a whole 4x4x4 slice. The times are simulated.
128 devices in a mesh: pair: 8 (over x_hi, y), aux: 16 (over x_lo, z, core).
Axes of the slice: x: 4 (x_hi: 2, x_lo: 2; x = x_hi * 2 + x_lo), y: 4, z: 4, core: 2. Of those that a mesh axis runs over, the one named last changes fastest.
Arguments:
- same_panels: bfloat16 [64, 2, 112, 59904], P('aux', None, None, 'pair'), may hold values from -1 to 1
- opposite_panels: bfloat16 [64, 2, 112, 59904], P('aux', None, None, 'pair'), may hold values from -1 to 1
- same_amplitudes: bfloat16 [64, 112, 112], replicated, may hold values from -2 to 2
- opposite_amplitudes: bfloat16 [64, 112, 112], replicated, may hold values from -2 to 2
- same_energies: float32 [64, 2, 112], replicated, may hold values from 0.5 to 3
- opposite_energies: float32 [64, 2, 112], replicated, may hold values from 0.5 to 3
- same_ranks: int32 [64], replicated, may hold values from 48 to 112
- opposite_ranks: int32 [64], replicated, may hold values from 48 to 112
Outputs:
- same_residual: float32 [64, 112, 112], P('pair', 'aux')
- opposite_residual: float32 [64, 112, 112], P('pair', 'aux')
Inputs may be any that keep to these rules, and one draw needn't show every extreme that they name: `same_ranks`: slots at or beyond a pair's rank are padding. `opposite_ranks`: slots at or beyond a pair's rank are padding.
All inputs are finite; a program needn't handle non-finite values.
Results may differ from a plain program's by a relative error of at most 0.0013.
Values may be sent and summed in bfloat16 or wider, within the bound.
A program may use at most 128 MiB of HBM per device.

v0:
```python
import jax
import jax.numpy as jnp
from jax import lax
from jax.sharding import PartitionSpec as P


def from_everyone(value, axis):
    peers = lax.axis_size(axis)
    return lax.all_to_all(
        jnp.broadcast_to(value[None], (peers, *value.shape)), axis, 0, 0, tiled=True
    )


def taken_together(value, axis):
    everything = from_everyone(value, axis)
    return jnp.sum(everything, axis=0)


def side_by_side(arrays, axis, split_dim, concat_dim, along):
    widths = [a.shape[along] for a in arrays]
    both = jnp.concatenate(arrays, axis=along)
    whole = lax.all_to_all(both, axis, split_axis=split_dim, concat_axis=concat_dim, tiled=True)
    return tuple(jnp.split(whole, [sum(widths[:k]) for k in range(1, len(widths))], axis=along))


def cut_along(value, dim, peers):
    dims = value.shape
    pieces = value.reshape(*dims[:dim], peers, dims[dim] // peers, *dims[dim + 1 :])
    return jnp.moveaxis(pieces, dim, 0)


def summed_on_arrival(value, axis, dim):
    peers = lax.axis_size(axis)
    pieces = lax.all_to_all(cut_along(value, dim, peers), axis, 0, 0, tiled=True)
    return jnp.sum(pieces, axis=0)


def side_by_side_2(arrays, axis, dim, along):
    widths = [a.shape[along] for a in arrays]
    both = jnp.concatenate(arrays, axis=along)
    whole = summed_on_arrival(both, axis, dim)
    return tuple(jnp.split(whole, [sum(widths[:k]) for k in range(1, len(widths))], axis=along))


def slot_mask(ranks, slots):
    places = jnp.arange(slots, dtype=jnp.int32)
    return (places[None, :] < ranks[:, None]).astype(jnp.float32)


def masked_amplitudes(amplitudes, keep):
    outer = keep[:, :, None] * keep[:, None, :]
    return (amplitudes.astype(jnp.float32) * outer).astype(jnp.bfloat16)


def dressing_total(panels, masked):
    mixed = jnp.einsum("pab,pbn->pan", masked, panels[:, 1], preferred_element_type=jnp.float32)
    return jnp.sum(panels[:, 0].astype(jnp.float32) * mixed, axis=(0, 1))


def partial_terms(panels, coupling):
    exchange = jnp.einsum(
        "pan,pbn->pab", panels[:, 0], panels[:, 1], preferred_element_type=jnp.float32
    )
    scaled = (panels[:, 0].astype(jnp.float32) * coupling[None, None, :]).astype(jnp.bfloat16)
    coulomb = jnp.einsum("pan,pbn->pab", scaled, panels[:, 1], preferred_element_type=jnp.float32)
    return exchange + coulomb


def finish_rows(summed, amplitudes, energies, ranks, pair_start, row_start):
    count = summed.shape[0]
    rows = summed.shape[1]
    slots = amplitudes.shape[1]
    keep = slot_mask(lax.dynamic_slice_in_dim(ranks, pair_start, count, 0), slots)
    amplitude = lax.dynamic_slice_in_dim(amplitudes, pair_start, count, 0)
    masked = masked_amplitudes(amplitude, keep)
    masked_rows = lax.dynamic_slice_in_dim(masked, row_start, rows, 1).astype(jnp.float32)
    energy = lax.dynamic_slice_in_dim(energies, pair_start, count, 0)
    first_gap = lax.dynamic_slice_in_dim(energy[:, 0], row_start, rows, 1)
    keep_rows = lax.dynamic_slice_in_dim(keep, row_start, rows, 1)
    diagonal = (first_gap[:, :, None] + energy[:, 1][:, None, :]) * masked_rows
    return (summed + diagonal) * (keep_rows[:, :, None] * keep[:, None, :])


def local_masked(amplitudes, ranks, start, count):
    slots = amplitudes.shape[1]
    keep = slot_mask(lax.dynamic_slice_in_dim(ranks, start, count, 0), slots)
    return masked_amplitudes(lax.dynamic_slice_in_dim(amplitudes, start, count, 0), keep)


def body(
    same_panels,
    opposite_panels,
    same_amplitudes,
    opposite_amplitudes,
    same_energies,
    opposite_energies,
    same_ranks,
    opposite_ranks,
):
    block_count = same_panels.shape[0]
    pair_index = lax.axis_index("pair")
    aux_index = lax.axis_index("aux")
    owned = block_count * lax.axis_size("aux") // lax.axis_size("pair")
    rows = same_amplitudes.shape[1] // lax.axis_size("aux")
    start = aux_index * block_count
    same_masked = local_masked(same_amplitudes, same_ranks, start, block_count)
    opposite_masked = local_masked(opposite_amplitudes, opposite_ranks, start, block_count)
    partial_coupling = dressing_total(same_panels, same_masked) + dressing_total(
        opposite_panels, opposite_masked
    )
    coupling = taken_together(partial_coupling, "aux")
    same_rows, opposite_rows = side_by_side(
        (partial_terms(same_panels, coupling), partial_terms(opposite_panels, coupling)),
        "aux",
        1,
        0,
        2,
    )
    same_sum, opposite_sum = side_by_side_2((same_rows, opposite_rows), "pair", 0, 1)
    pair_start = pair_index * owned
    row_start = aux_index * rows
    same_residual = finish_rows(
        same_sum, same_amplitudes, same_energies, same_ranks, pair_start, row_start
    )
    opposite_residual = finish_rows(
        opposite_sum, opposite_amplitudes, opposite_energies, opposite_ranks, pair_start, row_start
    )
    return (same_residual, opposite_residual)


def solution(mesh):
    placed = (
        P("aux", None, None, "pair"),
        P("aux", None, None, "pair"),
        P(),
        P(),
        P(),
        P(),
        P(),
        P(),
    )
    return jax.shard_map(
        body,
        mesh=mesh,
        in_specs=placed,
        out_specs=(P("pair", "aux", None), P("pair", "aux", None)),
        check_vma=False,
    )
```

profile of v0, /device:TPU:0, one launch (start us, length us, event | category | flops | bytes accessed | tf_op | source)
XLA Modules:
  0.0 92.9 jit_solution(15163469474702537182)
XLA Ops:
  0.6 0.7 dynamic_slice.51
  1.4 0.1 fusion.55
  1.4 0.7 dynamic_slice.49
  2.2 0.1 fusion.54
  2.2 0.0 copy-start
  2.2 7.1 %fusion.2 = f32[7488]{0:T(1024)S(1)} fusion(bf16[4,2,112,7488]{3,2,1,0:T(8,128)(2,1)} %param.9, f32[4,112]{1,0:T(4,128)S(1)} %fusion.55, bf16[64,112,112]{2,1,0:T(8,128)(2,1)} %param.11, s32[]{:T(128)S(6)} %select_n.6), kind=kOutput, calls=%fused_computation.6 | convolution fusion | flops 761692864 | bytes 13681924 | tf_op jit(solution)/shard_map/pab,pbn->pan/dot_general | solution.py:56
  9.3 1.7 %copy-done = bf16[4,2,112,7488]{3,2,1,0:T(8,128)(2,1)S(1)} copy-done((bf16[4,2,112,7488]{3,2,1,0:T(8,128)(2,1)S(1)}, bf16[4,2,112,7488]{3,2,1,0:T(8,128)(2,1)}, u32[]{:S(2)}) %copy-start) | copy-done | bytes 13418520
  11.0 0.0 copy-start.1
  11.0 0.0 copy-start.2
  11.0 3.2 %fusion = f32[7488]{0:T(1024)S(1)} fusion(bf16[4,2,112,7488]{3,2,1,0:T(8,128)(2,1)S(1)} %copy-done, f32[4,112]{1,0:T(4,128)S(1)} %fusion.54, bf16[64,112,112]{2,1,0:T(8,128)(2,1)} %param.10, s32[]{:T(128)S(6)} %select_n.6), kind=kOutput, calls=%fused_computation.4 | convolution fusion | flops 761692864 | bytes 13681924 | tf_op jit(solution)/shard_map/pab,pbn->pan/dot_general | solution.py:56
  14.2 1.0 %broadcast_in_dim.2 = f32[16,1,7488]{2,1,0:T(1,128)} broadcast(f32[7488]{0:T(1024)S(1)} %add.76), dimensions={2} | broadcast | bytes 509184 | tf_op jit(solution)/shard_map/broadcast_in_dim | solution.py:10
  15.2 6.5 %all-to-all-start = ((f32[16,1,7488]{2,1,0:T(1,128)}), f32[16,1,7488]{2,1,0:T(1,128)S(1)}, u32[]{:S(2)}, u32[]{:S(2)}) async-start(f32[16,1,7488]{2,1,0:T(1,128)} %broadcast_in_dim.2), calls=%async_computation | async-start | bytes 966656 | tf_op jit(solution)/shard_map/all_to_all | solution.py:9
  21.7 0.0 copy-done.1
  21.7 0.1 dynamic_slice.55
  21.8 0.0 copy-done.2
  21.8 0.1 dynamic_slice.61
  21.8 0.1 fusion.50
  21.9 10.1 %all-to-all-done = f32[16,1,7488]{2,1,0:T(1,128)S(1)} async-done(((f32[16,1,7488]{2,1,0:T(1,128)}), f32[16,1,7488]{2,1,0:T(1,128)S(1)}, u32[]{:S(2)}, u32[]{:S(2)}) %all-to-all-start) | async-done | bytes 479264 | tf_op jit(solution)/shard_map/all_to_all | solution.py:9
  32.1 0.3 reduce_sum.38
  32.4 6.8 %fusion.6 = f32[4,112,112]{1,2,0:T(8,128)S(1)} fusion(f32[7488]{0:T(1024)S(1)} %reduce_sum.38, bf16[4,2,112,7488]{3,2,1,0:T(8,128)(2,1)} %param.8), kind=kOutput, calls=%fused_computation.9 | convolution fusion | flops 761499648 | bytes 13649152 | tf_op jit(solution)/shard_map/pan,pbn->pab/dot_general | solution.py:65
  39.2 6.8 %fusion.4 = f32[4,112,112]{1,2,0:T(8,128)S(1)} fusion(f32[7488]{0:T(1024)S(1)} %reduce_sum.38, bf16[4,2,112,7488]{3,2,1,0:T(8,128)(2,1)} %param.9), kind=kOutput, calls=%fused_computation.8 | convolution fusion | flops 761499648 | bytes 13649152 | tf_op jit(solution)/shard_map/pan,pbn->pab/dot_general | solution.py:65
  46.0 6.8 %fusion.32 = f32[4,112,112]{1,2,0:T(8,128)S(1)} fusion(f32[4,112,112]{1,2,0:T(8,128)S(1)} %fusion.6, bf16[4,2,112,7488]{3,2,1,0:T(8,128)(2,1)} %param.8), kind=kOutput, calls=%fused_computation.34 | convolution fusion | flops 751485952 | bytes 13819904 | tf_op jit(solution)/shard_map/pan,pbn->pab/dot_general | solution.py:61
  52.8 6.8 %fusion.37 = f32[4,112,112]{1,2,0:T(8,128)S(1)} fusion(f32[4,112,112]{1,2,0:T(8,128)S(1)} %fusion.4, bf16[4,2,112,7488]{3,2,1,0:T(8,128)(2,1)} %param.9), kind=kOutput, calls=%fused_computation.35 | convolution fusion | flops 751485952 | bytes 13819904 | tf_op jit(solution)/shard_map/pan,pbn->pab/dot_general | solution.py:61
  59.7 1.0 %copy.79 = f32[4,112,224]{2,0,1:T(4,128)} copy(f32[4,112,224]{1,2,0:T(8,128)S(1)} %pad_maximum_fusion) | data formatting | bytes 802816 | tf_op jit(solution)/shard_map/concatenate | solution.py:21
  60.7 3.6 %all-to-all-start.1 = ((f32[4,112,224]{2,0,1:T(4,128)}), f32[4,112,224]{2,0,1:T(4,128)S(1)}, u32[]{:S(2)}, u32[]{:S(2)}) async-start(f32[4,112,224]{2,0,1:T(4,128)} %copy.79), calls=%async_computation.1 | async-start | bytes 917504 | tf_op jit(solution)/shard_map/all_to_all | solution.py:22
  64.2 0.1 fusion.51
  64.3 0.1 copy.85
  64.4 0.1 copy.90
  64.5 0.1 constant_dynamic-slice_fusion.2
  64.6 0.8 constant_dynamic-slice_fusion.5
  65.4 0.7 constant_dynamic-slice_fusion.6
  66.1 8.2 %all-to-all-done.1 = f32[4,112,224]{2,0,1:T(4,128)S(1)} async-done(((f32[4,112,224]{2,0,1:T(4,128)}), f32[4,112,224]{2,0,1:T(4,128)S(1)}, u32[]{:S(2)}, u32[]{:S(2)}) %all-to-all-start.1) | async-done | bytes 401440 | tf_op jit(solution)/shard_map/all_to_all | solution.py:22
  74.3 0.2 all_to_all.24
  74.5 0.1 fusion.56
  74.7 0.8 copy.81
  75.5 6.6 %all-to-all-start.2 = ((f32[8,8,14,112]{3,1,2,0:T(8,128)}), f32[8,8,14,112]{3,1,2,0:T(8,128)S(1)}, u32[]{:S(2)}, u32[]{:S(2)}) async-start(f32[8,8,14,112]{3,1,2,0:T(8,128)} %copy.81), calls=%async_computation.2 | async-start | bytes 917504 | tf_op jit(solution)/shard_map/all_to_all | solution.py:34
  82.1 0.1 copy.86
  82.2 0.1 copy.91
  82.3 0.1 copy.83
  82.4 0.1 copy.88
  82.5 1.1 %constant_dynamic-slice_fusion.4 = (bf16[8,112,112]{2,1,0:T(8,128)(2,1)S(1)}, bf16[8,112,112]{2,1,0:T(8,128)(2,1)S(1)}) fusion(bf16[64,112,112]{2,1,0:T(8,128)(2,1)} %param.11, s32[]{:T(128)S(6)} %select_n.7, bf16[64,112,112]{2,1,0:T(8,128)(2,1)} %param.10), kind=kLoop, calls=%fused_computation.60 | loop fusion | bytes 802820 | tf_op jit(solution)/shard_map/dynamic_slice | solution.py:74
  83.6 8.5 %all-to-all-done.2 = f32[8,8,14,112]{3,1,2,0:T(8,128)S(1)} async-done(((f32[8,8,14,112]{3,1,2,0:T(8,128)}), f32[8,8,14,112]{3,1,2,0:T(8,128)S(1)}, u32[]{:S(2)}, u32[]{:S(2)}) %all-to-all-start.2) | async-done | bytes 401440 | tf_op jit(solution)/shard_map/all_to_all | solution.py:34
  92.2 0.7 fusion.48
  (8 shorter events, 0.2 us)
Async XLA Ops:
  2.2 8.8 %copy-start = (bf16[4,2,112,7488]{3,2,1,0:T(8,128)(2,1)S(1)}, bf16[4,2,112,7488]{3,2,1,0:T(8,128)(2,1)}, u32[]{:S(2)}) copy-start(bf16[4,2,112,7488]{3,2,1,0:T(8,128)(2,1)} %param.8) | copy-start | bytes 40255492
  11.0 10.7 %copy-start.1 = (s32[64]{0:T(128)S(1)}, s32[64]{0:T(128)}, u32[]{:S(2)}) copy-start(s32[64]{0:T(128)} %param.14) | copy-start | bytes 772
  11.0 10.8 %copy-start.2 = (s32[64]{0:T(128)S(1)}, s32[64]{0:T(128)}, u32[]{:S(2)}) copy-start(s32[64]{0:T(128)} %param.15) | copy-start | bytes 772
  15.2 16.9 %all-to-all-start = ((f32[16,1,7488]{2,1,0:T(1,128)}), f32[16,1,7488]{2,1,0:T(1,128)S(1)}, u32[]{:S(2)}, u32[]{:S(2)}) async-start(f32[16,1,7488]{2,1,0:T(1,128)} %broadcast_in_dim.2), calls=%async_computation | async-start | bytes 966656 | tf_op jit(solution)/shard_map/all_to_all | solution.py:9
  60.7 13.7 %all-to-all-start.1 = ((f32[4,112,224]{2,0,1:T(4,128)}), f32[4,112,224]{2,0,1:T(4,128)S(1)}, u32[]{:S(2)}, u32[]{:S(2)}) async-start(f32[4,112,224]{2,0,1:T(4,128)} %copy.79), calls=%async_computation.1 | async-start | bytes 917504 | tf_op jit(solution)/shard_map/all_to_all | solution.py:22
  75.5 16.6 %all-to-all-start.2 = ((f32[8,8,14,112]{3,1,2,0:T(8,128)}), f32[8,8,14,112]{3,1,2,0:T(8,128)S(1)}, u32[]{:S(2)}, u32[]{:S(2)}) async-start(f32[8,8,14,112]{3,1,2,0:T(8,128)} %copy.81), calls=%async_computation.2 | async-start | bytes 917504 | tf_op jit(solution)/shard_map/all_to_all | solution.py:34
where the time goes:
time: 93.4 us; the launch traced here: 92.9 us
  matrix products  37.5 us (40%)
  waiting for transfers between devices  26.9 us (29%)
  starting transfers between devices  16.7 us (18%)
  local copies, waits for them, and re-layouts  9.64 us (10%)
  other arithmetic  1.46 us (2%)
    dot_general x2, matrix products, partial_terms(): jnp.einsum('pan,pbn->pab', panels[:, 0], panels[:, 1], preferred_element_...  13.6 us
    dot_general x2, matrix products, partial_terms(): jnp.einsum('pan,pbn->pab', scaled, panels[:, 1], preferred_element_type=j...  13.6 us
    dot_general x2, matrix products, dressing_total(): jnp.einsum('pab,pbn->pan', masked, panels[:, 1], preferred_element_type=j...  10.2 us
    all_to_all x1, waiting for transfers between devices, from_everyone(): lax.all_to_all(jnp.broadcast_to(value[None], (peers, *value.shape)), axis...  10.1 us
    all_to_all x1, waiting for transfers between devices, summed_on_arrival(): lax.all_to_all(cut_along(value, dim, peers), axis, 0, 0, tiled=True)  8.5 us
    all_to_all x1, waiting for transfers between devices, side_by_side(): lax.all_to_all(both, axis, split_axis=split_dim, concat_axis=concat_dim,...  8.23 us
    all_to_all x1, starting transfers between devices, summed_on_arrival(): lax.all_to_all(cut_along(value, dim, peers), axis, 0, 0, tiled=True)  6.63 us
    all_to_all x1, starting transfers between devices, from_everyone(): lax.all_to_all(jnp.broadcast_to(value[None], (peers, *value.shape)), axis...  6.46 us
  transfers between devices with their start and end apart: 3, of which 3 were waited for; matrix products, arithmetic and copies ran while one was open for 4% of the time, Pallas kernels for 0%

commit v1 on v0

v1 whole, which is shorter than its diff:
```python
import jax
import jax.numpy as jnp
from jax import lax
from jax.experimental import pallas as pl
from jax.experimental.pallas import tpu as pltpu
from jax.sharding import PartitionSpec as P

f32 = jnp.float32
bf16 = jnp.bfloat16
MESH = pl.DeviceIdType.MESH

R = 112
CHUNKS = ((0, 2048), (2048, 2048), (4096, 2048), (6144, 1344))
BLOCK = 1024
NT = (((1,), (1,)), ((), ()))


def tiles_of(width):
    return (width + 127) // 128


def kernel(
    sp, op, sa, oa, se, oe, sr, orr, out_s, out_o,
    pan0, pan1, pan2, pan3,
    raw, tm, famp, fen, fadd, fmask,
    cp0, cp1, cp2, cp3, cr0, cr1, cr2, cr3, cs,
    acc, sb1, rb1, sb2, rb2,
    pan_sem, raw_sem, fin_sem, c_send, c_recv, s1_send, s1_recv, s2_send, s2_recv,
):
    p = lax.axis_index("pair")
    a = lax.axis_index("aux")
    pan = (pan0, pan1, pan2, pan3)
    cps = (cp0, cp1, cp2, cp3)
    crs = (cr0, cr1, cr2, cr3)
    diagonal = p == a // 2

    raw_copies = [
        pltpu.make_async_copy(src.at[pl.ds(4 * a, 4)], raw.at[pl.ds(4 * s, 4)], raw_sem.at[s])
        for s, src in enumerate((sa, oa))
    ]
    for copy in raw_copies:
        copy.start()
    pan_copies = []
    for c, (start, width) in enumerate(CHUNKS):
        row = []
        for i in range(8):
            src = (sp if i < 4 else op).at[i % 4, :, :, pl.ds(start, width)]
            copy = pltpu.make_async_copy(src, pan[c].at[i], pan_sem.at[c, i])
            copy.start()
            row.append(copy)
        pan_copies.append(row)
    fin_copies = []
    for s, (amp, en) in enumerate(((sa, se), (oa, oe))):
        fin_copies.append(
            pltpu.make_async_copy(amp.at[pl.ds(8 * p, 8)], famp.at[pl.ds(8 * s, 8)], fin_sem.at[s])
        )
        fin_copies.append(
            pltpu.make_async_copy(en.at[pl.ds(8 * p, 8)], fen.at[pl.ds(8 * s, 8)], fin_sem.at[2 + s])
        )
    for copy in fin_copies:
        copy.start()

    barrier = pltpu.get_barrier_semaphore()
    for k in range(1, 16):
        pl.semaphore_signal(
            barrier, inc=1, device_id=(p, lax.rem(a + k, 16)), device_id_type=MESH
        )
    for k in range(1, 8):
        pl.semaphore_signal(barrier, inc=1, device_id=(lax.rem(p + k, 8), a), device_id_type=MESH)
    own = lax.rem(a, 2)
    for k in range(2):

        @pl.when(jnp.logical_not(jnp.logical_and(diagonal, own == k)))
        def _():
            pl.semaphore_signal(
                barrier, inc=1, device_id=(a // 2, 2 * p + k), device_id_type=MESH
            )

    for copy in raw_copies:
        copy.wait()
    rows_i = lax.broadcasted_iota(jnp.int32, (R, R), 0)
    cols_i = lax.broadcasted_iota(jnp.int32, (R, R), 1)
    for i in range(8):
        rank = (sr if i < 4 else orr)[4 * a + i % 4]
        kept = jnp.logical_and(rows_i < rank, cols_i < rank)
        tm[i] = jnp.where(kept, raw[i].astype(f32), 0.0).astype(bf16)

    def mixed(c):
        width = CHUNKS[c][1]

        def block(tile, offset, size):
            total = jnp.zeros((8, size), f32)
            for i in range(8):
                m = jnp.dot(
                    tm[i], pan[c][i, 1, :, pl.ds(offset, size)], preferred_element_type=f32
                )
                prod = m * pan[c][i, 0, :, pl.ds(offset, size)].astype(f32)
                total = total + jnp.sum(prod.reshape(14, 8, size), axis=0)
            line = jnp.sum(total, axis=0, keepdims=True)
            for k in range(tiles_of(size)):
                part = min(128, size - 128 * k)
                cps[c][pl.ds(tile + k, 1), 0:part] = line[:, 128 * k : 128 * k + part]

        full = width // BLOCK

        def step(n, carry):
            block(n * (BLOCK // 128), pl.multiple_of(n * BLOCK, BLOCK), BLOCK)
            return carry

        lax.fori_loop(0, full, step, 0)
        if width > full * BLOCK:
            block(full * (BLOCK // 128), full * BLOCK, width - full * BLOCK)

    def send_coupling(c):
        for k in range(1, 16):
            pltpu.make_async_remote_copy(
                src_ref=cps[c],
                dst_ref=crs[c].at[k - 1],
                send_sem=c_send.at[c],
                recv_sem=c_recv.at[c],
                device_id=(p, lax.rem(a + k, 16)),
                device_id_type=MESH,
            ).start()

    def take_coupling(c):
        pltpu.make_async_copy(crs[c], crs[c], c_recv.at[c]).wait()
        total = cps[c][...]
        for k in range(15):
            total = total + crs[c][k]
        cs[c] = total

    def exchange(c):
        for i in range(8):
            e = lax.dot_general(pan[c][i, 0], pan[c][i, 1], NT, preferred_element_type=f32)
            acc[i] = e if c == 0 else acc[i] + e

    def coulomb(c, i):
        width = CHUNKS[c][1]
        parts = []
        for t in range(tiles_of(width)):
            size = min(128, width - 128 * t)
            left = pan[c][i, 0, :, 128 * t : 128 * t + size].astype(f32)
            parts.append((left * cs[c, t : t + 1, 0:size]).astype(bf16))
        scaled = jnp.concatenate(parts, axis=1)
        return lax.dot_general(scaled, pan[c][i, 1], NT, preferred_element_type=f32)

    for c in range(4):
        cps[c][...] = jnp.zeros_like(cps[c])
        for i in range(8):
            pan_copies[c][i].wait()
        mixed(c)
        if c == 0:
            pl.semaphore_wait(barrier, 24 - diagonal.astype(jnp.int32))
        send_coupling(c)
        exchange(c)

    for c in range(3):
        take_coupling(c)
        for i in range(8):
            acc[i] = acc[i] + coulomb(c, i)

    for copy in fin_copies:
        copy.wait()
    sel_r = lax.broadcasted_iota(jnp.int32, (16, R), 0)
    sel_c = lax.broadcasted_iota(jnp.int32, (16, R), 1)
    first = 7 * a
    chosen = jnp.logical_and(sel_c == first + sel_r, sel_r < 7)
    select = chosen.astype(f32).astype(bf16)
    pick = chosen[0:8].astype(f32)
    for k in range(16):
        rank = (sr if k < 8 else orr)[8 * p + k % 8]
        amp = jnp.dot(select, famp[k], preferred_element_type=f32)[0:8]
        first_gap = jnp.sum(pick * fen[k, 0:1, :], axis=1, keepdims=True)
        kept = jnp.logical_and(first + sel_r[0:8] < rank, sel_c[0:8] < rank)
        fmask[k] = kept.astype(f32)
        fadd[k] = (first_gap + fen[k, 1:2, :]) * amp

    take_coupling(3)
    for s in range(2):
        for j in range(4):
            i = 4 * s + j
            total = acc[i] + coulomb(3, i)
            for d in range(8):
                sb1[d, s, 14 * j : 14 * j + 14, 0:R] = total[14 * d : 14 * d + 14]
        for k in range(1, 8):
            d = lax.rem(p + k, 8)
            pltpu.make_async_remote_copy(
                src_ref=sb1.at[d, s],
                dst_ref=rb1.at[s, k - 1],
                send_sem=s1_send.at[s],
                recv_sem=s1_recv.at[s],
                device_id=(d, a),
                device_id_type=MESH,
            ).start()

    for s in range(2):
        pltpu.make_async_copy(rb1.at[s], rb1.at[s], s1_recv.at[s]).wait()
        total = sb1[p, s]
        for k in range(7):
            total = total + rb1[s, k]
        for j in range(4):
            for q in range(2):
                sb2[q, s, j, 0:7, :] = total[14 * j + 7 * q : 14 * j + 7 * q + 7]
        for q in range(2):
            mine = jnp.logical_and(diagonal, own == q)

            @pl.when(mine)
            def _():
                rb2[q, s] = sb2[q, s]

            @pl.when(jnp.logical_not(mine))
            def _():
                pltpu.make_async_remote_copy(
                    src_ref=sb2.at[q, s],
                    dst_ref=rb2.at[own, s],
                    send_sem=s2_send.at[q, s],
                    recv_sem=s2_recv.at[own, s],
                    device_id=(a // 2, 2 * p + q),
                    device_id_type=MESH,
                ).start()

    for s, out in enumerate((out_s, out_o)):
        for b in range(2):

            @pl.when(jnp.logical_not(jnp.logical_and(diagonal, own == b)))
            def _():
                pltpu.make_async_copy(rb2.at[b, s], rb2.at[b, s], s2_recv.at[b, s]).wait()
                pltpu.make_async_copy(rb2.at[b, s], rb2.at[b, s], s2_send.at[b, s]).wait()

            for j in range(4):
                k = 8 * s + 4 * b + j
                value = (rb2[b, s, j, :, 0:R] + fadd[k]) * fmask[k]
                out[4 * b + j] = value[0:7]

    for c in range(4):
        pltpu.make_async_copy(crs[c], crs[c], c_send.at[c]).wait()
    for s in range(2):
        pltpu.make_async_copy(rb1.at[s], rb1.at[s], s1_send.at[s]).wait()


def body(sp, op, sa, oa, se, oe, sr, orr):
    any_space = pl.BlockSpec(memory_space=pl.ANY)
    smem = pl.BlockSpec(memory_space=pltpu.SMEM)
    vmem = pl.BlockSpec(memory_space=pltpu.VMEM)
    out = jax.ShapeDtypeStruct((8, 7, R), f32)
    rows = 16
    sem = pltpu.SemaphoreType.DMA
    return pl.pallas_call(
        kernel,
        out_shape=[out, out],
        in_specs=[any_space] * 6 + [smem] * 2,
        out_specs=[vmem, vmem],
        scratch_shapes=[pltpu.VMEM((8, 2, R, w), bf16) for _, w in CHUNKS]
        + [
            pltpu.VMEM((8, R, R), bf16),
            pltpu.VMEM((8, R, R), bf16),
            pltpu.VMEM((16, R, R), bf16),
            pltpu.VMEM((16, 2, R), f32),
            pltpu.VMEM((16, 8, R), f32),
            pltpu.VMEM((16, 8, R), f32),
        ]
        + [pltpu.VMEM((rows, 128), f32)] * 4
        + [pltpu.VMEM((15, rows, 128), f32)] * 4
        + [
            pltpu.VMEM((4, rows, 128), f32),
            pltpu.VMEM((8, R, R), f32),
            pltpu.VMEM((8, 2, 56, 128), f32),
            pltpu.VMEM((2, 7, 56, 128), f32),
            pltpu.VMEM((2, 2, 4, 8, 128), f32),
            pltpu.VMEM((2, 2, 4, 8, 128), f32),
            sem((4, 8)),
            sem((2,)),
            sem((4,)),
            sem((4,)),
            sem((4,)),
            sem((2,)),
            sem((2,)),
            sem((2, 2)),
            sem((2, 2)),
        ],
        compiler_params=pltpu.CompilerParams(
            collective_id=0, has_side_effects=True, vmem_limit_bytes=60 * 1024 * 1024
        ),
    )(sp, op, sa, oa, se, oe, sr, orr)


def solution(mesh):
    panels = P("aux", None, None, "pair")
    return jax.shard_map(
        body,
        mesh=mesh,
        in_specs=(panels, panels) + (P(),) * 6,
        out_specs=(P("pair", "aux", None), P("pair", "aux", None)),
        check_vma=False,
    )
```

time: 93.4 us -> 44.1 us (0.47)
  the two profiles are of different devices: /device:TPU:0 before, /device:TPU:17 now
where the time goes in v1:
time: 44.1 us; the launch traced here: 43.8 us
  Pallas kernels  40.4 us (92%)
  local copies, waits for them, and re-layouts  2.75 us (6%)
  between operations  0.64 us (1%)
    pallas_call x1, Pallas kernels, body(): pl.pallas_call(kernel, out_shape=[out, out], in_specs=[any_space] * 6 + [...  40.4 us
    pallas_call x2, local copies, waits for them, and re-layouts, body(): pl.pallas_call(kernel, out_shape=[out, out], in_specs=[any_space] * 6 + [...  2.75 us

profile of v1, /device:TPU:17, one launch (start us, length us, event | category | flops | bytes accessed | tf_op | source)
XLA Modules:
  0.0 43.8 jit_solution(17519500421632864226)
XLA Ops:
  0.6 40.4 %shard_map.95 = (f32[8,7,112]{2,1,0:T(8,128)}, f32[8,7,112]{2,1,0:T(8,128)}) custom-call(bf16[4,2,112,7488]{3,2,1,0:T(8,128)(2,1)} %sp.1, bf16[4,2,112,7488]{3,2,1,0:T(8,128)(2,1)} %op.1, bf16[64,112,112]{2,1,0:T(8,128)(2,1)} %sa.1, bf16[64,112,112]{2,1,0:T(8,128)(2,1)} %oa.1, f32[64,2,112]{2,1,0:T(2,128)} %se.1, f32[64,2,112]{2,1,0:T(2,128)} %oe.1, s32[64]{0:T(128)} %sr.1, ...), custom_call_target="tpu_custom_call" | custom-call | tf_op jit(solution)/shard_map/pallas_call | solution.py:248
  41.1 1.4 %copy.10 = f32[8,7,112]{2,0,1:T(8,128)} copy(f32[8,7,112]{2,1,0:T(8,128)} %get-tuple-element.2) | data formatting | bytes 50176 | tf_op jit(solution)/shard_map/pallas_call | solution.py:248
  42.4 1.4 %copy.11 = f32[8,7,112]{2,0,1:T(8,128)} copy(f32[8,7,112]{2,1,0:T(8,128)} %get-tuple-element.3) | data formatting | bytes 50176 | tf_op jit(solution)/shard_map/pallas_call | solution.py:248

commit v2 on v1

--- a/solution.py
+++ b/solution.py
@@ -10,8 +10,8 @@
 MESH = pl.DeviceIdType.MESH
 
 R = 112
-CHUNKS = ((0, 2048), (2048, 2048), (4096, 2048), (6144, 1344))
-BLOCK = 1024
+CHUNKS = ((0, 1024), (1024, 2048), (3072, 2304), (5376, 2112))
+N = len(CHUNKS)
 NT = (((1,), (1,)), ((), ()))
 
 
@@ -19,19 +19,20 @@
     return (width + 127) // 128
 
 
+def rows_of(width):
+    return (tiles_of(width) + 7) // 8 * 8
+
+
 def kernel(
-    sp, op, sa, oa, se, oe, sr, orr, out_s, out_o,
-    pan0, pan1, pan2, pan3,
-    raw, tm, famp, fen, fadd, fmask,
-    cp0, cp1, cp2, cp3, cr0, cr1, cr2, cr3, cs,
-    acc, sb1, rb1, sb2, rb2,
-    pan_sem, raw_sem, fin_sem, c_send, c_recv, s1_send, s1_recv, s2_send, s2_recv,
+    sp, op, sa, oa, se, oe, sr, orr, out_s, out_o, *scratch
 ):
+    pan, cps, crs, cs = (scratch[N * k : N * k + N] for k in range(4))
+    (
+        raw, tm, famp, fen, fadd, fmask, acc, tot, sb1, rb1, sb2, rb2,
+        pan_sem, raw_sem, fin_sem, c_send, c_recv, s1_send, s1_recv, s2_send, s2_recv,
+    ) = scratch[4 * N :]
     p = lax.axis_index("pair")
     a = lax.axis_index("aux")
-    pan = (pan0, pan1, pan2, pan3)
-    cps = (cp0, cp1, cp2, cp3)
-    crs = (cr0, cr1, cr2, cr3)
     diagonal = p == a // 2
 
     raw_copies = [
@@ -46,7 +47,7 @@
         for i in range(8):
             src = (sp if i < 4 else op).at[i % 4, :, :, pl.ds(start, width)]
             copy = pltpu.make_async_copy(src, pan[c].at[i], pan_sem.at[c, i])
-            copy.start()
+            copy.start(priority=1)
             row.append(copy)
         pan_copies.append(row)
     fin_copies = []
@@ -88,28 +89,15 @@
     def mixed(c):
         width = CHUNKS[c][1]
 
-        def block(tile, offset, size):
-            total = jnp.zeros((8, size), f32)
-            for i in range(8):
-                m = jnp.dot(
-                    tm[i], pan[c][i, 1, :, pl.ds(offset, size)], preferred_element_type=f32
-                )
-                prod = m * pan[c][i, 0, :, pl.ds(offset, size)].astype(f32)
-                total = total + jnp.sum(prod.reshape(14, 8, size), axis=0)
-            line = jnp.sum(total, axis=0, keepdims=True)
-            for k in range(tiles_of(size)):
-                part = min(128, size - 128 * k)
-                cps[c][pl.ds(tile + k, 1), 0:part] = line[:, 128 * k : 128 * k + part]
-
-        full = width // BLOCK
-
-        def step(n, carry):
-            block(n * (BLOCK // 128), pl.multiple_of(n * BLOCK, BLOCK), BLOCK)
-            return carry
-
-        lax.fori_loop(0, full, step, 0)
-        if width > full * BLOCK:
-            block(full * (BLOCK // 128), full * BLOCK, width - full * BLOCK)
+        total = jnp.zeros((8, width), f32)
+        for i in range(8):
+            m = jnp.dot(tm[i], pan[c][i, 1], preferred_element_type=f32)
+            prod = m * pan[c][i, 0].astype(f32)
+            total = total + jnp.sum(prod.reshape(14, 8, width), axis=0)
+        line = jnp.sum(total, axis=0, keepdims=True)
+        for k in range(tiles_of(width)):
+            part = min(128, width - 128 * k)
+            cps[c][k : k + 1, 0:part] = line[:, 128 * k : 128 * k + part]
 
     def send_coupling(c):
         for k in range(1, 16):
@@ -127,7 +115,7 @@
         total = cps[c][...]
         for k in range(15):
             total = total + crs[c][k]
-        cs[c] = total
+        cs[c][...] = total
 
     def exchange(c):
         for i in range(8):
@@ -140,11 +128,12 @@
         for t in range(tiles_of(width)):
             size = min(128, width - 128 * t)
             left = pan[c][i, 0, :, 128 * t : 128 * t + size].astype(f32)
-            parts.append((left * cs[c, t : t + 1, 0:size]).astype(bf16))
+            parts.append((left * cs[c][t : t + 1, 0:size]).astype(bf16))
         scaled = jnp.concatenate(parts, axis=1)
         return lax.dot_general(scaled, pan[c][i, 1], NT, preferred_element_type=f32)
 
-    for c in range(4):
+    tot[...] = jnp.zeros_like(tot)
+    for c in range(N):
         cps[c][...] = jnp.zeros_like(cps[c])
         for i in range(8):
             pan_copies[c][i].wait()
@@ -154,7 +143,7 @@
         send_coupling(c)
         exchange(c)
 
-    for c in range(3):
+    for c in range(N - 1):
         take_coupling(c)
         for i in range(8):
             acc[i] = acc[i] + coulomb(c, i)
@@ -171,17 +160,20 @@
         rank = (sr if k < 8 else orr)[8 * p + k % 8]
         amp = jnp.dot(select, famp[k], preferred_element_type=f32)[0:8]
         first_gap = jnp.sum(pick * fen[k, 0:1, :], axis=1, keepdims=True)
-        kept = jnp.logical_and(first + sel_r[0:8] < rank, sel_c[0:8] < rank)
-        fmask[k] = kept.astype(f32)
-        fadd[k] = (first_gap + fen[k, 1:2, :]) * amp
-
-    take_coupling(3)
+        kept = jnp.logical_and(first + sel_r[0:8] < rank, sel_c[0:8] < rank).astype(f32)
+        added = (first_gap + fen[k, 1:2, :]) * amp
+        for r in range(7):
+            fmask[k // 8, r, k % 8 : k % 8 + 1, :] = kept[r : r + 1]
+            fadd[k // 8, r, k % 8 : k % 8 + 1, :] = added[r : r + 1]
+
+    take_coupling(N - 1)
     for s in range(2):
         for j in range(4):
             i = 4 * s + j
-            total = acc[i] + coulomb(3, i)
+            total = acc[i] + coulomb(N - 1, i)
+            tot[i, :, 0:R] = total
             for d in range(8):
-                sb1[d, s, 14 * j : 14 * j + 14, 0:R] = total[14 * d : 14 * d + 14]
+                sb1[d, s, pl.ds(j, 14, stride=4), :] = tot[i, 14 * d : 14 * d + 14, :]
         for k in range(1, 8):
             d = lax.rem(p + k, 8)
             pltpu.make_async_remote_copy(
@@ -198,9 +190,8 @@
         total = sb1[p, s]
         for k in range(7):
             total = total + rb1[s, k]
-        for j in range(4):
-            for q in range(2):
-                sb2[q, s, j, 0:7, :] = total[14 * j + 7 * q : 14 * j + 7 * q + 7]
+        for r in range(14):
+            sb2[r // 7, s, r % 7] = total[4 * r : 4 * r + 4]
         for q in range(2):
             mine = jnp.logical_and(diagonal, own == q)
 
@@ -227,52 +218,54 @@
                 pltpu.make_async_copy(rb2.at[b, s], rb2.at[b, s], s2_recv.at[b, s]).wait()
                 pltpu.make_async_copy(rb2.at[b, s], rb2.at[b, s], s2_send.at[b, s]).wait()
 
-            for j in range(4):
-                k = 8 * s + 4 * b + j
-                value = (rb2[b, s, j, :, 0:R] + fadd[k]) * fmask[k]
-                out[4 * b + j] = value[0:7]
-
-    for c in range(4):
+        for r in range(7):
+            value = jnp.concatenate([rb2[0, s, r, :, 0:R], rb2[1, s, r, :, 0:R]], axis=0)
+            out[r] = (value + fadd[s, r]) * fmask[s, r]
+
+    for c in range(N):
         pltpu.make_async_copy(crs[c], crs[c], c_send.at[c]).wait()
     for s in range(2):
         pltpu.make_async_copy(rb1.at[s], rb1.at[s], s1_send.at[s]).wait()
+
+
+def hand_out(same, opposite, out_s, out_o):
+    out_s[...] = same[...]
+    out_o[...] = opposite[...]
 
 
 def body(sp, op, sa, oa, se, oe, sr, orr):
     any_space = pl.BlockSpec(memory_space=pl.ANY)
     smem = pl.BlockSpec(memory_space=pltpu.SMEM)
     vmem = pl.BlockSpec(memory_space=pltpu.VMEM)
-    out = jax.ShapeDtypeStruct((8, 7, R), f32)
-    rows = 16
+    out = jax.ShapeDtypeStruct((7, 8, R), f32)
     sem = pltpu.SemaphoreType.DMA
-    return pl.pallas_call(
+    same, opposite = pl.pallas_call(
         kernel,
         out_shape=[out, out],
         in_specs=[any_space] * 6 + [smem] * 2,
         out_specs=[vmem, vmem],
         scratch_shapes=[pltpu.VMEM((8, 2, R, w), bf16) for _, w in CHUNKS]
+        + [pltpu.VMEM((rows_of(w), 128), f32) for _, w in CHUNKS]
+        + [pltpu.VMEM((15, rows_of(w), 128), f32) for _, w in CHUNKS]
+        + [pltpu.VMEM((rows_of(w), 128), f32) for _, w in CHUNKS]
         + [
             pltpu.VMEM((8, R, R), bf16),
             pltpu.VMEM((8, R, R), bf16),
             pltpu.VMEM((16, R, R), bf16),
             pltpu.VMEM((16, 2, R), f32),
-            pltpu.VMEM((16, 8, R), f32),
-            pltpu.VMEM((16, 8, R), f32),
-        ]
-        + [pltpu.VMEM((rows, 128), f32)] * 4
-        + [pltpu.VMEM((15, rows, 128), f32)] * 4
-        + [
-            pltpu.VMEM((4, rows, 128), f32),
+            pltpu.VMEM((2, 7, 8, R), f32),
+            pltpu.VMEM((2, 7, 8, R), f32),
             pltpu.VMEM((8, R, R), f32),
+            pltpu.VMEM((8, R, 128), f32),
             pltpu.VMEM((8, 2, 56, 128), f32),
             pltpu.VMEM((2, 7, 56, 128), f32),
-            pltpu.VMEM((2, 2, 4, 8, 128), f32),
-            pltpu.VMEM((2, 2, 4, 8, 128), f32),
-            sem((4, 8)),
+            pltpu.VMEM((2, 2, 7, 4, 128), f32),
+            pltpu.VMEM((2, 2, 7, 4, 128), f32),
+            sem((N, 8)),
             sem((2,)),
             sem((4,)),
-            sem((4,)),
-            sem((4,)),
+            sem((N,)),
+            sem((N,)),
             sem((2,)),
             sem((2,)),
             sem((2, 2)),
@@ -282,6 +275,13 @@
             collective_id=0, has_side_effects=True, vmem_limit_bytes=60 * 1024 * 1024
         ),
     )(sp, op, sa, oa, se, oe, sr, orr)
+    same, opposite = pl.pallas_call(
+        hand_out,
+        out_shape=[out, out],
+        in_specs=[vmem, vmem],
+        out_specs=[vmem, vmem],
+    )(same, opposite)
+    return jnp.transpose(same, (1, 0, 2)), jnp.transpose(opposite, (1, 0, 2))
 
 
 def solution(mesh):

time: 44.1 us -> 36.2 us (0.82)
  Pallas kernels: 40.4 us -> 35.3 us
  local copies, waits for them, and re-layouts: 2.75 us -> 0 us
    pallas_call x1, Pallas kernels: 40.4 us -> 33.9 us  [body(): pl.pallas_call(kernel, out_shape=[out, out], in_specs=[any_space] * 6 + [...]
    pallas_call x2 -> x0, local copies, waits for them, and re-layouts: 2.75 us -> none  [body(): pl.pallas_call(kernel, out_shape=[out, out], in_specs=[any_space] * 6 + [...]
    pallas_call x0 -> x1, Pallas kernels: none -> 1.39 us  [body(): pl.pallas_call(hand_out, out_shape=[out, out], in_specs=[vmem, vmem], out...]
where the time goes in v2:
time: 36.2 us; the launch traced here: 35.9 us
  Pallas kernels  35.3 us (98%)
  between operations  0.64 us (2%)
    pallas_call x1, Pallas kernels, body(): pl.pallas_call(kernel, out_shape=[out, out], in_specs=[any_space] * 6 + [...  33.9 us
    pallas_call x1, Pallas kernels, body(): pl.pallas_call(hand_out, out_shape=[out, out], in_specs=[vmem, vmem], out...  1.39 us

profile of v2, /device:TPU:17, one launch (start us, length us, event | category | flops | bytes accessed | tf_op | source)
XLA Modules:
  0.0 35.9 jit_solution(10731987552720421670)
XLA Ops:
  0.6 33.9 %shard_map.95 = (f32[7,8,112]{2,1,0:T(8,128)}, f32[7,8,112]{2,1,0:T(8,128)}) custom-call(bf16[4,2,112,7488]{3,2,1,0:T(8,128)(2,1)} %sp.1, bf16[4,2,112,7488]{3,2,1,0:T(8,128)(2,1)} %op.1, bf16[64,112,112]{2,1,0:T(8,128)(2,1)} %sa.1, bf16[64,112,112]{2,1,0:T(8,128)(2,1)} %oa.1, f32[64,2,112]{2,1,0:T(2,128)} %se.1, f32[64,2,112]{2,1,0:T(2,128)} %oe.1, s32[64]{0:T(128)} %sr.1, ...), custom_call_target="tpu_custom_call" | custom-call | tf_op jit(solution)/shard_map/pallas_call | solution.py:242
  34.6 1.4 %shard_map.96 = (f32[7,8,112]{2,1,0:T(8,128)}, f32[7,8,112]{2,1,0:T(8,128)}) custom-call(f32[7,8,112]{2,1,0:T(8,128)} %get-tuple-element.6.same, f32[7,8,112]{2,1,0:T(8,128)} %get-tuple-element.7.opposite), custom_call_target="tpu_custom_call" | custom-call | tf_op jit(solution)/shard_map/pallas_call | solution.py:278

commit v3 on v2

--- a/solution.py
+++ b/solution.py
@@ -10,8 +10,10 @@
 MESH = pl.DeviceIdType.MESH
 
 R = 112
-CHUNKS = ((0, 1024), (1024, 2048), (3072, 2304), (5376, 2112))
+CHUNKS = ((0, 1024), (1024, 1792), (2816, 2048), (4864, 1664), (6528, 960))
 N = len(CHUNKS)
+HELD = 3
+LATE = 4
 NT = (((1,), (1,)), ((), ()))
 
 
@@ -133,7 +135,9 @@
         return lax.dot_general(scaled, pan[c][i, 1], NT, preferred_element_type=f32)
 
     tot[...] = jnp.zeros_like(tot)
-    for c in range(N):
+    tot[...] = jnp.zeros_like(tot)
+
+    def prepare(c):
         cps[c][...] = jnp.zeros_like(cps[c])
         for i in range(8):
             pan_copies[c][i].wait()
@@ -141,9 +145,15 @@
         if c == 0:
             pl.semaphore_wait(barrier, 24 - diagonal.astype(jnp.int32))
         send_coupling(c)
+
+    for c in range(N):
+        prepare(c)
+        if c < N - HELD:
+            exchange(c)
+    for c in range(N - HELD, N):
         exchange(c)
 
-    for c in range(N - 1):
+    for c in range(N - LATE):
         take_coupling(c)
         for i in range(8):
             acc[i] = acc[i] + coulomb(c, i)
@@ -166,11 +176,14 @@
             fmask[k // 8, r, k % 8 : k % 8 + 1, :] = kept[r : r + 1]
             fadd[k // 8, r, k % 8 : k % 8 + 1, :] = added[r : r + 1]
 
-    take_coupling(N - 1)
+    for c in range(N - LATE, N):
+        take_coupling(c)
     for s in range(2):
         for j in range(4):
             i = 4 * s + j
-            total = acc[i] + coulomb(N - 1, i)
+            total = acc[i]
+            for c in range(N - LATE, N):
+                total = total + coulomb(c, i)
             tot[i, :, 0:R] = total
             for d in range(8):
                 sb1[d, s, pl.ds(j, 14, stride=4), :] = tot[i, 14 * d : 14 * d + 14, :]
@@ -239,6 +252,9 @@
     vmem = pl.BlockSpec(memory_space=pltpu.VMEM)
     out = jax.ShapeDtypeStruct((7, 8, R), f32)
     sem = pltpu.SemaphoreType.DMA
+    sp, op, sa, oa, se, oe, sr, orr = (
+        pltpu.with_memory_space_constraint(x, pltpu.HBM) for x in (sp, op, sa, oa, se, oe, sr, orr)
+    )
     same, opposite = pl.pallas_call(
         kernel,
         out_shape=[out, out],
@@ -272,7 +288,7 @@
             sem((2, 2)),
         ],
         compiler_params=pltpu.CompilerParams(
-            collective_id=0, has_side_effects=True, vmem_limit_bytes=60 * 1024 * 1024
+            collective_id=0, has_side_effects=True, vmem_limit_bytes=52 * 1024 * 1024
         ),
     )(sp, op, sa, oa, se, oe, sr, orr)
     same, opposite = pl.pallas_call(
@@ -280,6 +296,7 @@
         out_shape=[out, out],
         in_specs=[vmem, vmem],
         out_specs=[vmem, vmem],
+        compiler_params=pltpu.CompilerParams(vmem_limit_bytes=1024 * 1024),
     )(same, opposite)
     return jnp.transpose(same, (1, 0, 2)), jnp.transpose(opposite, (1, 0, 2))
 

time: 36.2 us -> 34.4 us (0.950)
  Pallas kernels: 35.3 us -> 33.7 us
    pallas_call x1, Pallas kernels: 33.9 us -> 33 us  [body(): pl.pallas_call(kernel, out_shape=[out, out], in_specs=[any_space] * 6 + [...]
    pallas_call x1, Pallas kernels: 1.39 us -> 0.62 us  [body(): pl.pallas_call(hand_out, out_shape=[out, out], in_specs=[vmem, vmem], out...]
where the time goes in v3:
time: 34.4 us; the launch traced here: 34.3 us
  Pallas kernels  33.7 us (98%)
  between operations  0.64 us (2%)
    pallas_call x1, Pallas kernels, body(): pl.pallas_call(kernel, out_shape=[out, out], in_specs=[any_space] * 6 + [...  33 us

profile of v3, /device:TPU:17, one launch (start us, length us, event | category | flops | bytes accessed | tf_op | source)
XLA Modules:
  0.0 34.3 jit_solution(17448595895217517908)
XLA Ops:
  0.6 33.0 %shard_map.95 = (f32[7,8,112]{2,1,0:T(8,128)S(1)}, f32[7,8,112]{2,1,0:T(8,128)S(1)}) custom-call(bf16[4,2,112,7488]{3,2,1,0:T(8,128)(2,1)} %sp.1, bf16[4,2,112,7488]{3,2,1,0:T(8,128)(2,1)} %op.1, bf16[64,112,112]{2,1,0:T(8,128)(2,1)} %sa.1, bf16[64,112,112]{2,1,0:T(8,128)(2,1)} %oa.1, f32[64,2,112]{2,1,0:T(2,128)} %se.1, f32[64,2,112]{2,1,0:T(2,128)} %oe.1, ...), custom_call_target="tpu_custom_call" | custom-call | tf_op jit(solution)/shard_map/pallas_call | solution.py:258
  33.7 0.6 %shard_map.96 = (f32[7,8,112]{2,1,0:T(8,128)}, f32[7,8,112]{2,1,0:T(8,128)}) custom-call(f32[7,8,112]{2,1,0:T(8,128)S(1)} %get-tuple-element.6.same, f32[7,8,112]{2,1,0:T(8,128)S(1)} %get-tuple-element.7.opposite), custom_call_target="tpu_custom_call" | custom-call | tf_op jit(solution)/shard_map/pallas_call | solution.py:294

commit v4 on v3

--- a/solution.py
+++ b/solution.py
@@ -157,24 +157,6 @@
         take_coupling(c)
         for i in range(8):
             acc[i] = acc[i] + coulomb(c, i)
-
-    for copy in fin_copies:
-        copy.wait()
-    sel_r = lax.broadcasted_iota(jnp.int32, (16, R), 0)
-    sel_c = lax.broadcasted_iota(jnp.int32, (16, R), 1)
-    first = 7 * a
-    chosen = jnp.logical_and(sel_c == first + sel_r, sel_r < 7)
-    select = chosen.astype(f32).astype(bf16)
-    pick = chosen[0:8].astype(f32)
-    for k in range(16):
-        rank = (sr if k < 8 else orr)[8 * p + k % 8]
-        amp = jnp.dot(select, famp[k], preferred_element_type=f32)[0:8]
-        first_gap = jnp.sum(pick * fen[k, 0:1, :], axis=1, keepdims=True)
-        kept = jnp.logical_and(first + sel_r[0:8] < rank, sel_c[0:8] < rank).astype(f32)
-        added = (first_gap + fen[k, 1:2, :]) * amp
-        for r in range(7):
-            fmask[k // 8, r, k % 8 : k % 8 + 1, :] = kept[r : r + 1]
-            fadd[k // 8, r, k % 8 : k % 8 + 1, :] = added[r : r + 1]
 
     for c in range(N - LATE, N):
         take_coupling(c)
@@ -198,6 +180,24 @@
                 device_id_type=MESH,
             ).start()
 
+    for copy in fin_copies:
+        copy.wait()
+    sel_r = lax.broadcasted_iota(jnp.int32, (16, R), 0)
+    sel_c = lax.broadcasted_iota(jnp.int32, (16, R), 1)
+    first = 7 * a
+    chosen = jnp.logical_and(sel_c == first + sel_r, sel_r < 7)
+    select = chosen.astype(f32).astype(bf16)
+    pick = chosen[0:8].astype(f32)
+    for k in range(16):
+        rank = (sr if k < 8 else orr)[8 * p + k % 8]
+        amp = jnp.dot(select, famp[k], preferred_element_type=f32)[0:8]
+        first_gap = jnp.sum(pick * fen[k, 0:1, :], axis=1, keepdims=True)
+        kept = jnp.logical_and(first + sel_r[0:8] < rank, sel_c[0:8] < rank).astype(f32)
+        added = (first_gap + fen[k, 1:2, :]) * amp
+        for r in range(7):
+            fmask[k // 8, r, k % 8 : k % 8 + 1, :] = kept[r : r + 1]
+            fadd[k // 8, r, k % 8 : k % 8 + 1, :] = added[r : r + 1]
+
     for s in range(2):
         pltpu.make_async_copy(rb1.at[s], rb1.at[s], s1_recv.at[s]).wait()
         total = sb1[p, s]
@@ -241,9 +241,15 @@
         pltpu.make_async_copy(rb1.at[s], rb1.at[s], s1_send.at[s]).wait()
 
 
-def hand_out(same, opposite, out_s, out_o):
-    out_s[...] = same[...]
-    out_o[...] = opposite[...]
+def hand_out(same, opposite, out_s, out_o, sem):
+    copies = [
+        pltpu.make_async_copy(src, dst, sem.at[k])
+        for k, (src, dst) in enumerate(((same, out_s), (opposite, out_o)))
+    ]
+    for copy in copies:
+        copy.start()
+    for copy in copies:
+        copy.wait()
 
 
 def body(sp, op, sa, oa, se, oe, sr, orr):
@@ -295,7 +301,8 @@
         hand_out,
         out_shape=[out, out],
         in_specs=[vmem, vmem],
-        out_specs=[vmem, vmem],
+        out_specs=[any_space, any_space],
+        scratch_shapes=[sem((2,))],
         compiler_params=pltpu.CompilerParams(vmem_limit_bytes=1024 * 1024),
     )(same, opposite)
     return jnp.transpose(same, (1, 0, 2)), jnp.transpose(opposite, (1, 0, 2))

time: 34.4 us -> 34.4 us (level)
  no operation moved by 1% of the time
where the time goes in v4:
time: 34.4 us; the launch traced here: 34.3 us
  Pallas kernels  33.7 us (98%)
  between operations  0.64 us (2%)
    pallas_call x1, Pallas kernels, body(): pl.pallas_call(kernel, out_shape=[out, out], in_specs=[any_space] * 6 + [...  33 us

profile of v4, /device:TPU:17, one launch (start us, length us, event | category | flops | bytes accessed | tf_op | source)
XLA Modules:
  0.0 34.3 jit_solution(13060484566699424843)
XLA Ops:
  0.6 33.0 %shard_map.95 = (f32[7,8,112]{2,1,0:T(8,128)S(1)}, f32[7,8,112]{2,1,0:T(8,128)S(1)}) custom-call(bf16[4,2,112,7488]{3,2,1,0:T(8,128)(2,1)} %sp.1, bf16[4,2,112,7488]{3,2,1,0:T(8,128)(2,1)} %op.1, bf16[64,112,112]{2,1,0:T(8,128)(2,1)} %sa.1, bf16[64,112,112]{2,1,0:T(8,128)(2,1)} %oa.1, f32[64,2,112]{2,1,0:T(2,128)} %se.1, f32[64,2,112]{2,1,0:T(2,128)} %oe.1, ...), custom_call_target="tpu_custom_call" | custom-call | tf_op jit(solution)/shard_map/pallas_call | solution.py:264
  33.7 0.6 %shard_map.96 = (f32[7,8,112]{2,1,0:T(8,128)}, f32[7,8,112]{2,1,0:T(8,128)}) custom-call(f32[7,8,112]{2,1,0:T(8,128)S(1)} %get-tuple-element.6.same, f32[7,8,112]{2,1,0:T(8,128)S(1)} %get-tuple-element.7.opposite), custom_call_target="tpu_custom_call" | custom-call | tf_op jit(solution)/shard_map/pallas_call | solution.py:300
